TPU v7x, 32 devices: a whole 2x2x4 slice. The times are simulated.
32 devices in a mesh: patch: 8 (over z, x), member: 4 (over y, core).
Axes of the slice: x: 2, y: 2, z: 4, core: 2. Of those that a mesh axis runs over, the one named last changes fastest.
Arguments:
- background: bfloat16 [32, 16, 3, 64, 128], P('patch', None, None, 'member'), may hold values from -6 to 6
- patch_blocks: int32 [32], replicated, may hold values from 1 to 16, as said below
- obs_values: float32 [16384], P(('patch', 'member')), may hold values from -12 to 12
- obs_errors: float32 [16384], P(('patch', 'member')), may hold values from 0.5 to 2
- obs_patch: int32 [16384], P('patch'), may hold values from 0 to 3
- obs_position: int32 [16384], P('patch'), may hold values from 0 to 1073741823
Outputs:
- analysis: bfloat16 [32, 16, 3, 64, 128], P('patch', None, None, 'member')
- inflation: float32 [], replicated
Inputs may be any that keep to these rules, and one draw needn't show every extreme that they name: `obs_patch`: index among the 4 patches held by the observation's index of patch. `patch_blocks`: the used blocks of the 4 patches of one index of patch sum to at most 32; some index reaches 32, and some patch uses all 16.
All inputs are finite; a program needn't handle non-finite values.
Results may differ from a plain program's by a relative error of at most 0.0065.
Values may be sent and summed in bfloat16 or wider, within the bound.
A program may use at most 64 MiB of HBM per device.

v0:
```python
import math
import jax
import jax.numpy as jnp
from jax import lax
from jax.sharding import PartitionSpec as P

K = 64
CB = 128
MAXB = 16
NS_STEPS = 4
PD = 4
OBS_DEV = 2048
neighbour_weight = 0.5


def extended(array, sides, width):
    for axis, dim in sides:
        count, length = (lax.axis_size(axis), array.shape[dim])
        up = [(i, (i + 1) % count) for i in range(count - 1)]
        down = [(j, i) for i, j in up]
        last = lax.slice_in_dim(array, length - width, length, axis=dim)
        initial = lax.slice_in_dim(array, 0, width, axis=dim)
        before = lax.ppermute(last, axis, up)
        after = lax.ppermute(initial, axis, down)
        array = jnp.concatenate([before, array, after], axis=dim)
    return array


def inverse_root(system):
    precise = lax.Precision.HIGHEST
    identity = jnp.eye(K, dtype=jnp.float32)
    norm_value = jnp.sqrt(jnp.sum(system * system, axis=(1, 2)))
    square_part = system / norm_value[:, None, None]
    inverse_part = jnp.broadcast_to(identity, system.shape)
    for sweep_index in range(NS_STEPS):
        middle = 1.5 * identity - 0.5 * jnp.einsum(
            "pij,pjk->pik", inverse_part, square_part, precision=precise
        )
        square_part = jnp.einsum("pij,pjk->pik", square_part, middle, precision=precise)
        inverse_part = jnp.einsum("pij,pjk->pik", middle, inverse_part, precision=precise)
    return inverse_part / jnp.sqrt(norm_value)[:, None, None]


def per_device(background, patch_blocks, obs_values, obs_errors, obs_patch, obs_position):
    precise = lax.Precision.HIGHEST
    member_count = lax.axis_size("member")
    local_members = K // member_count
    obs_share = OBS_DEV // member_count
    block_share = MAXB // member_count
    member_index = lax.axis_index("member")
    first_patch = lax.axis_index("patch") * PD
    used_blocks = lax.dynamic_slice_in_dim(patch_blocks, first_patch, PD)
    slot_table = jnp.arange(PD, dtype=jnp.int32)
    onehot_all = obs_patch[None, :] == slot_table[:, None]
    obs_counts = jnp.sum(jnp.where(onehot_all, used_blocks[:, None], 0), axis=0)
    cell_index = obs_position % (obs_counts * CB)
    flat_index = obs_patch * (MAXB * CB) + cell_index
    thickness = jnp.transpose(background[:, :, 0], (0, 1, 3, 2)).reshape(
        PD * MAXB * CB, local_members
    )
    sampled_local = thickness[flat_index]
    sampled = lax.all_to_all(sampled_local, "member", split_axis=0, concat_axis=1, tiled=True)
    own_slots = lax.dynamic_slice_in_dim(obs_patch, member_index * obs_share, obs_share)
    values = sampled.astype(jnp.float32)
    obs_mean = jnp.sum(values, axis=1) / K
    spread = values - obs_mean[:, None]
    innovation = obs_values - obs_mean
    variance = jnp.sum(spread * spread, axis=1) / (K - 1)
    misfit_part = jnp.sum(innovation * innovation)
    spread_part = jnp.sum(variance + obs_errors * obs_errors)
    weighted = spread / obs_errors[:, None]
    onehot = (own_slots[None, :] == slot_table[:, None]).astype(jnp.float32)
    masked = onehot[:, :, None] * weighted[None]
    gram_own = jnp.einsum("pjk,jl->pkl", masked, weighted, precision=precise)
    cross_own = jnp.einsum("pjk,j->pk", masked, innovation / obs_errors, precision=precise)
    stacked = jnp.concatenate([gram_own, cross_own[:, None, :]], axis=1)
    summed, misfit_member, spread_member = lax.psum((stacked, misfit_part, spread_part), "member")
    numerator, denominator = lax.psum((misfit_member, spread_member), "patch")
    inflation = numerator / denominator
    rimmed = extended(summed, (("patch", 0),), 1)
    localized = rimmed[1:-1] + neighbour_weight * (rimmed[:-2] + rimmed[2:])
    gram_local = localized[:, :K]
    cross_local = localized[:, K]
    identity = jnp.eye(K, dtype=jnp.float32)
    system = (K - 1) / inflation * identity + gram_local
    root_inverse = inverse_root(system)
    inner_weights = jnp.einsum("pkl,pl->pk", root_inverse, cross_local, precision=precise)
    mean_weights = jnp.einsum("pkl,pl->pk", root_inverse, inner_weights, precision=precise)
    transform = (mean_weights[:, :, None] + math.sqrt(K - 1) * root_inverse).astype(jnp.bfloat16)
    columns = lax.all_to_all(background, "member", split_axis=1, concat_axis=3, tiled=True)
    member_mean = jnp.sum(columns.astype(jnp.float32), axis=3) / K
    anomaly = (columns.astype(jnp.float32) - member_mean[:, :, :, None, :]).astype(jnp.bfloat16)
    combined = jnp.einsum(
        "pbvlc,plk->pbvkc", anomaly, transform, preferred_element_type=jnp.float32
    )
    block_ids = member_index * block_share + jnp.arange(block_share, dtype=jnp.int32)
    in_use = (block_ids[None, :] < used_blocks[:, None])[:, :, None, None, None]
    result = jnp.where(in_use, member_mean[:, :, :, None, :] + combined, 0.0).astype(jnp.bfloat16)
    analysis = lax.all_to_all(result, "member", split_axis=3, concat_axis=1, tiled=True)
    return (analysis, inflation)


def solution(mesh):
    in_specs = (
        P("patch", None, None, "member", None),
        P(),
        P(("patch", "member")),
        P(("patch", "member")),
        P("patch"),
        P("patch"),
    )
    out_specs = (P("patch", None, None, "member", None), P())
    return jax.shard_map(
        per_device, mesh=mesh, in_specs=in_specs, out_specs=out_specs, check_vma=False
    )
```

profile of v0, /device:TPU:0, one launch (start us, length us, event | category | flops | bytes accessed | tf_op | source)
XLA Modules:
  0.0 108.1 jit_solution(4150788410182912282)
XLA Ops:
  7.2 1.0 slice_bitcast_fusion
  8.2 1.0 copy.84
  9.6 6.2 %gather_fusion = bf16[2048,16]{1,0:T(8,128)(2,1)S(1)} fusion(bf16[8192,16]{1,0:T(8,128)(2,1)S(1)} %bitcast.75, s32[2048]{0:T(1024)S(1)} %fusion.30), kind=kCustom, calls=%fused_computation | custom fusion | bytes 139264 | tf_op jit(solution)/shard_map/gather | solution.py:61
  15.8 0.8 copy.85
  16.6 4.3 %all-to-all-start.1 = ((bf16[4,512,16]{1,2,0:T(8,128)(2,1)}), bf16[4,512,16]{1,2,0:T(8,128)(2,1)S(1)}, u32[]{:S(2)}, u32[]{:S(2)}) async-start(bf16[4,512,16]{1,2,0:T(8,128)(2,1)} %copy.85), calls=%async_computation.1 | async-start | bytes 131072 | tf_op jit(solution)/shard_map/all_to_all | solution.py:62
  21.0 1.0 copy.79
  22.0 2.9 %all-to-all-done.1 = bf16[4,512,16]{1,2,0:T(8,128)(2,1)S(1)} async-done(((bf16[4,512,16]{1,2,0:T(8,128)(2,1)}), bf16[4,512,16]{1,2,0:T(8,128)(2,1)S(1)}, u32[]{:S(2)}, u32[]{:S(2)}) %all-to-all-start.1) | async-done | bytes 65568 | tf_op jit(solution)/shard_map/all_to_all | solution.py:62
  25.0 3.5 %all-to-all-start = ((bf16[4,16,3,16,128]{4,3,2,0,1:T(8,128)(2,1)}), bf16[4,16,3,16,128]{4,3,2,0,1:T(8,128)(2,1)S(1)}, u32[]{:S(2)}, u32[]{:S(2)}) async-start(bf16[4,16,3,16,128]{4,3,2,0,1:T(8,128)(2,1)} %copy.79), calls=%async_computation | async-start | bytes 1572864 | tf_op jit(solution)/shard_map/all_to_all | solution.py:90
  28.6 0.7 multiply_reduce_fusion.2
  29.3 0.9 fusion.7
  30.2 0.6 convolution_bitcast_fusion
  30.7 0.8 pad_maximum_fusion.2
  31.7 10.3 %all-reduce.1 = (f32[]{:T(128)}, f32[]{:T(128)}) all-reduce(f32[]{:T(128)} %get-tuple-element.10, f32[]{:T(128)} %get-tuple-element.8), channel_id=1, replica_groups=mesh['patch'=8,'member'=4] {'member'}, use_global_device_ids=true, to_apply=%region_6.7 | all-reduce | flops 2 | bytes 16 | tf_op jit(solution)/shard_map/psum | solution.py:77
  42.0 22.8 %all-reduce = (f32[]{:T(128)}, f32[]{:T(128)}) all-reduce(f32[]{:T(128)} %get-tuple-element.4, f32[]{:T(128)} %get-tuple-element.5), channel_id=1, replica_groups=mesh['patch'=8,'member'=4] {'patch'}, use_global_device_ids=true, to_apply=%region_7.8 | all-reduce | flops 2 | bytes 16 | tf_op jit(solution)/shard_map/psum | solution.py:78
  66.2 0.8 fusion.36
  67.0 2.8 %collective-permute-start = (f32[1,65,64]{1,2,0:T(8,128)S(1)}, f32[1,65,64]{1,2,0:T(8,128)S(1)}, u32[]{:S(2)}, u32[]{:S(2)}) collective-permute-start(f32[1,65,64]{1,2,0:T(8,128)S(1)} %get-tuple-element.6), channel_id=1, source_target_pairs={{0,4},{4,8},{8,12},{12,16},{16,20},{20,24},{24,28},{1,5},{5,9},{9,... | collective-permute-start | bytes 49928 | tf_op jit(solution)/shard_map/ppermute | solution.py:23
  69.8 1.3 %collective-permute-start.1 = (f32[1,65,64]{1,2,0:T(8,128)S(1)}, f32[1,65,64]{1,2,0:T(8,128)S(1)}, u32[]{:S(2)}, u32[]{:S(2)}) collective-permute-start(f32[1,65,64]{1,2,0:T(8,128)S(1)} %get-tuple-element.7), channel_id=1, source_target_pairs={{4,0},{8,4},{12,8},{16,12},{20,16},{24,20},{28,24},{5,1},{9,5},{13... | collective-permute-start | bytes 49928 | tf_op jit(solution)/shard_map/ppermute | solution.py:24
  71.3 4.2 %collective-permute-done.1 = f32[1,65,64]{1,2,0:T(8,128)S(1)} collective-permute-done((f32[1,65,64]{1,2,0:T(8,128)S(1)}, f32[1,65,64]{1,2,0:T(8,128)S(1)}, u32[]{:S(2)}, u32[]{:S(2)}) %collective-permute-start.1) | collective-permute-done | bytes 16672 | tf_op jit(solution)/shard_map/ppermute | solution.py:24
  75.6 1.1 %fusion.15 = f32[4,65,64]{1,2,0:T(8,128)S(1)} fusion(f32[4,65,64]{1,2,0:T(8,128)} %all-reduce.4.cloned.1.call-done, f32[1,65,64]{1,2,0:T(8,128)S(1)} %collective-permute-done.1, f32[1,65,64]{1,2,0:T(8,128)S(1)} %collective-permute-done), kind=kLoop, calls=%fused_computation.30 | loop fusion | flops 83200 | bytes 166400 | tf_op jit(solution)/shard_map/add | solution.py:81
  81.9 0.5 fusion.1
  82.4 1.5 %copy.92 = bf16[4,4,3,64,128]{4,1,2,0,3:T(4,128)(2,1)} copy(bf16[4,4,3,64,128]{4,3,2,1,0:T(8,128)(2,1)S(1)} %fusion.1) | data formatting | bytes 1572864 | tf_op jit(solution)/shard_map/convert_element_type | solution.py:98
  83.9 3.5 %all-to-all-start.2 = ((bf16[4,4,3,64,128]{4,1,2,0,3:T(4,128)(2,1)}), bf16[4,4,3,64,128]{4,1,2,0,3:T(4,128)(2,1)S(1)}, u32[]{:S(2)}, u32[]{:S(2)}) async-start(bf16[4,4,3,64,128]{4,1,2,0,3:T(4,128)(2,1)} %copy.92), calls=%async_computation.2 | async-start | bytes 1572864 | tf_op jit(solution)/shard_map/all_to_all | solution.py:99
  88.7 10.3 %all-to-all-done.2 = bf16[4,4,3,64,128]{4,1,2,0,3:T(4,128)(2,1)S(1)} async-done(((bf16[4,4,3,64,128]{4,1,2,0,3:T(4,128)(2,1)}), bf16[4,4,3,64,128]{4,1,2,0,3:T(4,128)(2,1)S(1)}, u32[]{:S(2)}, u32[]{:S(2)}) %all-to-all-start.2) | async-done | bytes 786464 | tf_op jit(solution)/shard_map/all_to_all | solution.py:99
  99.0 1.1 %copy.93 = bf16[4,4,4,3,16,128]{5,4,3,2,1,0:T(8,128)(2,1)} copy(bf16[4,4,4,3,16,128]{5,2,3,0,4,1:T(4,128)(2,1)S(1)} %bitcast.77) | data formatting | bytes 1572864 | tf_op jit(solution)/shard_map/all_to_all | solution.py:99
  (56 shorter events, 6.3 us)
Async XLA Ops:
  7.2 2.1 %copy-start.5 = (s32[32]{0:T(128)S(1)}, s32[32]{0:T(128)}, u32[]{:S(2)}) copy-start(s32[32]{0:T(128)} %param.7) | copy-start | bytes 388
  7.2 2.1 %copy-start.1 = (s32[2048]{0:T(1024)S(1)}, s32[2048]{0:T(1024)}, u32[]{:S(2)}) copy-start(s32[2048]{0:T(1024)} %param.10) | copy-start | bytes 24580
  7.2 2.2 %copy-start.3 = (s32[2048]{0:T(1024)S(1)}, s32[2048]{0:T(1024)}, u32[]{:S(2)}) copy-start(s32[2048]{0:T(1024)} %param.11) | copy-start | bytes 24580
  9.6 11.4 %copy-start = (bf16[4,16,3,16,128]{4,3,2,1,0:T(8,128)(2,1)S(1)}, bf16[4,16,3,16,128]{4,3,2,1,0:T(8,128)(2,1)}, u32[]{:S(2)}) copy-start(bf16[4,16,3,16,128]{4,3,2,1,0:T(8,128)(2,1)} %param.6) | copy-start | bytes 2359300
  16.6 8.4 %all-to-all-start.1 = ((bf16[4,512,16]{1,2,0:T(8,128)(2,1)}), bf16[4,512,16]{1,2,0:T(8,128)(2,1)S(1)}, u32[]{:S(2)}, u32[]{:S(2)}) async-start(bf16[4,512,16]{1,2,0:T(8,128)(2,1)} %copy.85), calls=%async_computation.1 | async-start | bytes 131072 | tf_op jit(solution)/shard_map/all_to_all | solution.py:62
  21.0 7.6 %copy-start.2 = (f32[512]{0:T(512)S(1)}, f32[512]{0:T(512)}, u32[]{:S(2)}) copy-start(f32[512]{0:T(512)} %param.9) | copy-start | bytes 6148
  21.0 7.6 %copy-start.4 = (f32[512]{0:T(512)S(1)}, f32[512]{0:T(512)}, u32[]{:S(2)}) copy-start(f32[512]{0:T(512)} %param.8) | copy-start | bytes 6148
  25.0 55.9 %all-to-all-start = ((bf16[4,16,3,16,128]{4,3,2,0,1:T(8,128)(2,1)}), bf16[4,16,3,16,128]{4,3,2,0,1:T(8,128)(2,1)S(1)}, u32[]{:S(2)}, u32[]{:S(2)}) async-start(bf16[4,16,3,16,128]{4,3,2,0,1:T(8,128)(2,1)} %copy.79), calls=%async_computation | async-start | bytes 1572864 | tf_op jit(solution)/shard_map/all_to_all | solution.py:90
  28.5 37.7 %all-reduce.4.cloned.1.call-start = ((), (), s32[]{:S(2)}) async-start(), calls=%async_computation.3 | async-start | bytes 262144 | tf_op jit(solution)/shard_map/psum | solution.py:77
  67.0 4.4 %collective-permute-start = (f32[1,65,64]{1,2,0:T(8,128)S(1)}, f32[1,65,64]{1,2,0:T(8,128)S(1)}, u32[]{:S(2)}, u32[]{:S(2)}) collective-permute-start(f32[1,65,64]{1,2,0:T(8,128)S(1)} %get-tuple-element.6), channel_id=1, source_target_pairs={{0,4},{4,8},{8,12},{12,16},{16,20},{20,24},{24,28},{1,5},{5,9},{9,... | collective-permute-start | bytes 49928 | tf_op jit(solution)/shard_map/ppermute | solution.py:23
  69.8 5.8 %collective-permute-start.1 = (f32[1,65,64]{1,2,0:T(8,128)S(1)}, f32[1,65,64]{1,2,0:T(8,128)S(1)}, u32[]{:S(2)}, u32[]{:S(2)}) collective-permute-start(f32[1,65,64]{1,2,0:T(8,128)S(1)} %get-tuple-element.7), channel_id=1, source_target_pairs={{4,0},{8,4},{12,8},{16,12},{20,16},{24,20},{28,24},{5,1},{9,5},{13... | collective-permute-start | bytes 49928 | tf_op jit(solution)/shard_map/ppermute | solution.py:24
  83.9 15.1 %all-to-all-start.2 = ((bf16[4,4,3,64,128]{4,1,2,0,3:T(4,128)(2,1)}), bf16[4,4,3,64,128]{4,1,2,0,3:T(4,128)(2,1)S(1)}, u32[]{:S(2)}, u32[]{:S(2)}) async-start(bf16[4,4,3,64,128]{4,1,2,0,3:T(4,128)(2,1)} %copy.92), calls=%async_computation.2 | async-start | bytes 1572864 | tf_op jit(solution)/shard_map/all_to_all | solution.py:99
Sparse Core Ops, SparseCore 0:
  31.6 33.9 all-reduce.3
where the time goes:
time: 109 us; the launch traced here: 108 us
  blocking collectives  33.1 us (30%)
  between operations  18.1 us (17%)
  waiting for transfers between devices  17.7 us (16%)
  starting transfers between devices  15.4 us (14%)
  local copies, waits for them, and re-layouts  14.1 us (13%)
  matrix products  5.75 us (5%)
  other arithmetic  3.89 us (4%)
    psum x1, blocking collectives, per_device(): numerator, denominator = lax.psum((misfit_member, spread_member), 'patch')  22.8 us
    psum x1, blocking collectives, per_device(): lax.psum((stacked, misfit_part, spread_part), 'member')  10.3 us
    all_to_all x1, waiting for transfers between devices, per_device(): lax.all_to_all(result, 'member', split_axis=3, concat_axis=1, tiled=True)  10.3 us
    gather x1, local copies, waits for them, and re-layouts, per_device(): sampled_local = thickness[flat_index]  6.18 us
    all_to_all x1, starting transfers between devices, per_device(): lax.all_to_all(sampled_local, 'member', split_axis=0, concat_axis=1, tile...  4.26 us
    ppermute x1, waiting for transfers between devices, extended(): after = lax.ppermute(initial, axis, down)  4.23 us
    all_to_all x1, starting transfers between devices, per_device(): lax.all_to_all(background, 'member', split_axis=1, concat_axis=3, tiled=T...  3.49 us
    all_to_all x1, starting transfers between devices, per_device(): lax.all_to_all(result, 'member', split_axis=3, concat_axis=1, tiled=True)  3.49 us
  transfers between devices with their start and end apart: 6, of which 4 were waited for; matrix products, arithmetic and copies ran while one was open for 10% of the time, Pallas kernels for 0%

commit v1 on v0

--- a/solution.py
+++ b/solution.py
@@ -96,7 +96,20 @@
     block_ids = member_index * block_share + jnp.arange(block_share, dtype=jnp.int32)
     in_use = (block_ids[None, :] < used_blocks[:, None])[:, :, None, None, None]
     result = jnp.where(in_use, member_mean[:, :, :, None, :] + combined, 0.0).astype(jnp.bfloat16)
-    analysis = lax.all_to_all(result, "member", split_axis=3, concat_axis=1, tiled=True)
+    x_next, low = (lax.axis_size("member"), lax.axis_index("member"))
+    front = result.shape[3] // x_next
+    v1 = list(result.shape)
+    v1[3] = front
+    g_now = v1[1]
+    v1[1] = g_now * x_next
+    analysis = jnp.zeros(v1, result.dtype)
+    for k in range(x_next):
+        clean = lax.dynamic_slice_in_dim(result, (low ^ k) * front, front, axis=3)
+        if k:
+            clean = lax.ppermute(
+                clean, axis_name="member", perm=[(p, p ^ k) for p in range(x_next)]
+            )
+        analysis = lax.dynamic_update_slice_in_dim(analysis, clean, (low ^ k) * g_now, axis=1)
     return (analysis, inflation)
 
 

time: 109 us -> 104 us (0.954)
  starting transfers between devices: 15.4 us -> 13.8 us
  waiting for transfers between devices: 17.7 us -> 16.4 us
  local copies, waits for them, and re-layouts: 14.1 us -> 12.8 us
    all_to_all x1 -> x0, waiting for transfers between devices: 10.3 us -> none  [per_device(): lax.all_to_all(result, 'member', split_axis=3, concat_axis=1, tiled=True)]
    ppermute x0 -> x3, waiting for transfers between devices: none -> 8.93 us  [per_device(): lax.ppermute(clean, axis_name='member', perm=[(p, p ^ k) for p in range(x...]
    all_to_all x1 -> x0, starting transfers between devices: 3.49 us -> none  [per_device(): lax.all_to_all(result, 'member', split_axis=3, concat_axis=1, tiled=True)]
    ppermute x0 -> x3, starting transfers between devices: none -> 1.97 us  [per_device(): lax.ppermute(clean, axis_name='member', perm=[(p, p ^ k) for p in range(x...]
    convert_element_type x1 -> x0, local copies, waits for them, and re-layouts: 1.49 us -> none  [per_device(): jnp.where(in_use, member_mean[:, :, :, None, :] + combined, 0.0)]
  transfers between devices with their start and end apart: 6 -> 8, of which waited for: 4 -> 5; matrix products, arithmetic and copies ran while one was open for 10% -> 10% of each run, Pallas kernels for 0% -> 0%
where the time goes in v1:
time: 104 us
  blocking collectives  33.1 us (32%)
  between operations  18.2 us (18%)
  waiting for transfers between devices  16.4 us (16%)
  starting transfers between devices  13.8 us (13%)
  local copies, waits for them, and re-layouts  12.8 us (12%)
  matrix products  5.74 us (6%)
  other arithmetic  3.9 us (4%)
    psum x1, blocking collectives, per_device(): numerator, denominator = lax.psum((misfit_member, spread_member), 'patch')  22.8 us
    psum x1, blocking collectives, per_device(): lax.psum((stacked, misfit_part, spread_part), 'member')  10.3 us
    ppermute x3, waiting for transfers between devices, per_device(): lax.ppermute(clean, axis_name='member', perm=[(p, p ^ k) for p in range(x...  8.93 us
    gather x1, local copies, waits for them, and re-layouts, per_device(): sampled_local = thickness[flat_index]  6.18 us
    all_to_all x1, starting transfers between devices, per_device(): lax.all_to_all(sampled_local, 'member', split_axis=0, concat_axis=1, tile...  4.26 us
    ppermute x1, waiting for transfers between devices, extended(): after = lax.ppermute(initial, axis, down)  4.23 us
    all_to_all x1, starting transfers between devices, per_device(): lax.all_to_all(background, 'member', split_axis=1, concat_axis=3, tiled=T...  3.49 us
    all_to_all x1, waiting for transfers between devices, per_device(): lax.all_to_all(sampled_local, 'member', split_axis=0, concat_axis=1, tile...  2.91 us
  transfers between devices with their start and end apart: 8, of which 5 were waited for; matrix products, arithmetic and copies ran while one was open for 10% of the time, Pallas kernels for 0%

profile of v1, /device:TPU:0, one launch (start us, length us, event | category | flops | bytes accessed | tf_op | source)
XLA Modules:
  0.0 104.0 jit_solution(3360559319683197288)
XLA Ops:
  7.2 1.0 slice_bitcast_fusion
  8.2 1.0 copy.74
  9.6 6.2 %gather_fusion = bf16[2048,16]{1,0:T(8,128)(2,1)S(1)} fusion(bf16[8192,16]{1,0:T(8,128)(2,1)S(1)} %bitcast.77, s32[2048]{0:T(1024)S(1)} %fusion.29), kind=kCustom, calls=%fused_computation | custom fusion | bytes 139264 | tf_op jit(solution)/shard_map/gather | solution.py:61
  15.8 0.8 copy.75
  16.6 4.3 %all-to-all-start.1 = ((bf16[4,512,16]{1,2,0:T(8,128)(2,1)}), bf16[4,512,16]{1,2,0:T(8,128)(2,1)S(1)}, u32[]{:S(2)}, u32[]{:S(2)}) async-start(bf16[4,512,16]{1,2,0:T(8,128)(2,1)} %copy.75), calls=%async_computation.1 | async-start | bytes 131072 | tf_op jit(solution)/shard_map/all_to_all | solution.py:62
  21.0 1.0 copy.69
  22.0 2.9 %all-to-all-done.1 = bf16[4,512,16]{1,2,0:T(8,128)(2,1)S(1)} async-done(((bf16[4,512,16]{1,2,0:T(8,128)(2,1)}), bf16[4,512,16]{1,2,0:T(8,128)(2,1)S(1)}, u32[]{:S(2)}, u32[]{:S(2)}) %all-to-all-start.1) | async-done | bytes 65568 | tf_op jit(solution)/shard_map/all_to_all | solution.py:62
  25.0 3.5 %all-to-all-start = ((bf16[4,16,3,16,128]{4,3,2,0,1:T(8,128)(2,1)}), bf16[4,16,3,16,128]{4,3,2,0,1:T(8,128)(2,1)S(1)}, u32[]{:S(2)}, u32[]{:S(2)}) async-start(bf16[4,16,3,16,128]{4,3,2,0,1:T(8,128)(2,1)} %copy.69), calls=%async_computation | async-start | bytes 1572864 | tf_op jit(solution)/shard_map/all_to_all | solution.py:90
  28.6 0.7 multiply_reduce_fusion.2
  29.3 0.9 fusion.6
  30.2 0.5 convolution_bitcast_fusion
  30.7 0.8 pad_maximum_fusion.2
  31.7 10.3 %all-reduce.1 = (f32[]{:T(128)}, f32[]{:T(128)}) all-reduce(f32[]{:T(128)} %get-tuple-element.13, f32[]{:T(128)} %get-tuple-element.11), channel_id=1, replica_groups=mesh['patch'=8,'member'=4] {'member'}, use_global_device_ids=true, to_apply=%region_6.7 | all-reduce | flops 2 | bytes 16 | tf_op jit(solution)/shard_map/psum | solution.py:77
  42.0 22.8 %all-reduce = (f32[]{:T(128)}, f32[]{:T(128)}) all-reduce(f32[]{:T(128)} %get-tuple-element.4, f32[]{:T(128)} %get-tuple-element.5), channel_id=1, replica_groups=mesh['patch'=8,'member'=4] {'patch'}, use_global_device_ids=true, to_apply=%region_7.8 | all-reduce | flops 2 | bytes 16 | tf_op jit(solution)/shard_map/psum | solution.py:78
  66.2 0.8 fusion.35
  67.0 2.8 %collective-permute-start = (f32[1,65,64]{1,2,0:T(8,128)S(1)}, f32[1,65,64]{1,2,0:T(8,128)S(1)}, u32[]{:S(2)}, u32[]{:S(2)}) collective-permute-start(f32[1,65,64]{1,2,0:T(8,128)S(1)} %get-tuple-element.9), channel_id=1, source_target_pairs={{0,4},{4,8},{8,12},{12,16},{16,20},{20,24},{24,28},{1,5},{5,9},{9,... | collective-permute-start | bytes 49928 | tf_op jit(solution)/shard_map/ppermute | solution.py:23
  69.7 1.3 %collective-permute-start.1 = (f32[1,65,64]{1,2,0:T(8,128)S(1)}, f32[1,65,64]{1,2,0:T(8,128)S(1)}, u32[]{:S(2)}, u32[]{:S(2)}) collective-permute-start(f32[1,65,64]{1,2,0:T(8,128)S(1)} %get-tuple-element.10), channel_id=1, source_target_pairs={{4,0},{8,4},{12,8},{16,12},{20,16},{24,20},{28,24},{5,1},{9,5},{13... | collective-permute-start | bytes 49928 | tf_op jit(solution)/shard_map/ppermute | solution.py:24
  71.3 4.2 %collective-permute-done.1 = f32[1,65,64]{1,2,0:T(8,128)S(1)} collective-permute-done((f32[1,65,64]{1,2,0:T(8,128)S(1)}, f32[1,65,64]{1,2,0:T(8,128)S(1)}, u32[]{:S(2)}, u32[]{:S(2)}) %collective-permute-start.1) | collective-permute-done | bytes 16672 | tf_op jit(solution)/shard_map/ppermute | solution.py:24
  75.6 1.1 %fusion.14 = f32[4,65,64]{1,2,0:T(8,128)S(1)} fusion(f32[4,65,64]{1,2,0:T(8,128)} %all-reduce.4.cloned.1.call-done, f32[1,65,64]{1,2,0:T(8,128)S(1)} %collective-permute-done.1, f32[1,65,64]{1,2,0:T(8,128)S(1)} %collective-permute-done), kind=kLoop, calls=%fused_computation.33 | loop fusion | flops 83200 | bytes 166400 | tf_op jit(solution)/shard_map/add | solution.py:81
  84.0 0.6 collective-permute-start.3
  84.6 1.3 %collective-permute-start.4 = (bf16[4,4,3,16,128]{4,3,2,1,0:T(8,128)(2,1)S(1)}, bf16[4,4,3,16,128]{4,3,2,1,0:T(8,128)(2,1)S(1)}, u32[]{:S(2)}, u32[]{:S(2)}) collective-permute-start(bf16[4,4,3,16,128]{4,3,2,1,0:T(8,128)(2,1)S(1)} %get-tuple-element.6), channel_id=1, source_target_pairs={{0,3},{1,2},{2,1},{3,0},{4,7},{5,6},{6,5},{7,4},{8,11},{9,10},{10,... | collective-permute-start | bytes 589832 | tf_op jit(solution)/shard_map/ppermute | solution.py:109
  86.1 5.7 %collective-permute-done.3 = bf16[4,4,3,16,128]{4,3,2,1,0:T(8,128)(2,1)S(1)} collective-permute-done((bf16[4,4,3,16,128]{4,3,2,1,0:T(8,128)(2,1)S(1)}, bf16[4,4,3,16,128]{4,3,2,1,0:T(8,128)(2,1)S(1)}, u32[]{:S(2)}, u32[]{:S(2)}) %collective-permute-start.3) | collective-permute-done | bytes 196640 | tf_op jit(solution)/shard_map/ppermute | solution.py:109
  91.9 3.2 %collective-permute-done.4 = bf16[4,4,3,16,128]{4,3,2,1,0:T(8,128)(2,1)S(1)} collective-permute-done((bf16[4,4,3,16,128]{4,3,2,1,0:T(8,128)(2,1)S(1)}, bf16[4,4,3,16,128]{4,3,2,1,0:T(8,128)(2,1)S(1)}, u32[]{:S(2)}, u32[]{:S(2)}) %collective-permute-start.4) | collective-permute-done | bytes 196640 | tf_op jit(solution)/shard_map/ppermute | solution.py:109
  95.1 0.9 copy-done.1
  (66 shorter events, 7.2 us)
Async XLA Ops:
  7.2 2.1 %copy-start.6 = (s32[32]{0:T(128)S(1)}, s32[32]{0:T(128)}, u32[]{:S(2)}) copy-start(s32[32]{0:T(128)} %param.7) | copy-start | bytes 388
  7.2 2.1 %copy-start.2 = (s32[2048]{0:T(1024)S(1)}, s32[2048]{0:T(1024)}, u32[]{:S(2)}) copy-start(s32[2048]{0:T(1024)} %param.10) | copy-start | bytes 24580
  7.2 2.2 %copy-start.4 = (s32[2048]{0:T(1024)S(1)}, s32[2048]{0:T(1024)}, u32[]{:S(2)}) copy-start(s32[2048]{0:T(1024)} %param.11) | copy-start | bytes 24580
  9.6 11.4 %copy-start = (bf16[4,16,3,16,128]{4,3,2,1,0:T(8,128)(2,1)S(1)}, bf16[4,16,3,16,128]{4,3,2,1,0:T(8,128)(2,1)}, u32[]{:S(2)}) copy-start(bf16[4,16,3,16,128]{4,3,2,1,0:T(8,128)(2,1)} %param.6) | copy-start | bytes 2359300
  16.6 8.4 %all-to-all-start.1 = ((bf16[4,512,16]{1,2,0:T(8,128)(2,1)}), bf16[4,512,16]{1,2,0:T(8,128)(2,1)S(1)}, u32[]{:S(2)}, u32[]{:S(2)}) async-start(bf16[4,512,16]{1,2,0:T(8,128)(2,1)} %copy.75), calls=%async_computation.1 | async-start | bytes 131072 | tf_op jit(solution)/shard_map/all_to_all | solution.py:62
  21.0 7.6 %copy-start.3 = (f32[512]{0:T(512)S(1)}, f32[512]{0:T(512)}, u32[]{:S(2)}) copy-start(f32[512]{0:T(512)} %param.9) | copy-start | bytes 6148
  21.0 7.6 %copy-start.5 = (f32[512]{0:T(512)S(1)}, f32[512]{0:T(512)}, u32[]{:S(2)}) copy-start(f32[512]{0:T(512)} %param.8) | copy-start | bytes 6148
  25.0 55.9 %all-to-all-start = ((bf16[4,16,3,16,128]{4,3,2,0,1:T(8,128)(2,1)}), bf16[4,16,3,16,128]{4,3,2,0,1:T(8,128)(2,1)S(1)}, u32[]{:S(2)}, u32[]{:S(2)}) async-start(bf16[4,16,3,16,128]{4,3,2,0,1:T(8,128)(2,1)} %copy.69), calls=%async_computation | async-start | bytes 1572864 | tf_op jit(solution)/shard_map/all_to_all | solution.py:90
  28.5 37.7 %all-reduce.4.cloned.1.call-start = ((), (), s32[]{:S(2)}) async-start(), calls=%async_computation.2 | async-start | bytes 262144 | tf_op jit(solution)/shard_map/psum | solution.py:77
  67.0 4.4 %collective-permute-start = (f32[1,65,64]{1,2,0:T(8,128)S(1)}, f32[1,65,64]{1,2,0:T(8,128)S(1)}, u32[]{:S(2)}, u32[]{:S(2)}) collective-permute-start(f32[1,65,64]{1,2,0:T(8,128)S(1)} %get-tuple-element.9), channel_id=1, source_target_pairs={{0,4},{4,8},{8,12},{12,16},{16,20},{20,24},{24,28},{1,5},{5,9},{9,... | collective-permute-start | bytes 49928 | tf_op jit(solution)/shard_map/ppermute | solution.py:23
  69.7 5.8 %collective-permute-start.1 = (f32[1,65,64]{1,2,0:T(8,128)S(1)}, f32[1,65,64]{1,2,0:T(8,128)S(1)}, u32[]{:S(2)}, u32[]{:S(2)}) collective-permute-start(f32[1,65,64]{1,2,0:T(8,128)S(1)} %get-tuple-element.10), channel_id=1, source_target_pairs={{4,0},{8,4},{12,8},{16,12},{20,16},{24,20},{28,24},{5,1},{9,5},{13... | collective-permute-start | bytes 49928 | tf_op jit(solution)/shard_map/ppermute | solution.py:24
  82.6 3.5 %collective-permute-start.2 = (bf16[4,4,3,16,128]{4,3,2,1,0:T(8,128)(2,1)S(1)}, bf16[4,4,3,16,128]{4,3,2,1,0:T(8,128)(2,1)S(1)}, u32[]{:S(2)}, u32[]{:S(2)}) collective-permute-start(bf16[4,4,3,16,128]{4,3,2,1,0:T(8,128)(2,1)S(1)} %get-tuple-element.8), channel_id=1, source_target_pairs={{0,1},{1,0},{2,3},{3,2},{4,5},{5,4},{6,7},{7,6},{8,9},{9,8},{10,11... | collective-permute-start | bytes 589832 | tf_op jit(solution)/shard_map/ppermute | solution.py:109
  84.0 7.8 %collective-permute-start.3 = (bf16[4,4,3,16,128]{4,3,2,1,0:T(8,128)(2,1)S(1)}, bf16[4,4,3,16,128]{4,3,2,1,0:T(8,128)(2,1)S(1)}, u32[]{:S(2)}, u32[]{:S(2)}) collective-permute-start(bf16[4,4,3,16,128]{4,3,2,1,0:T(8,128)(2,1)S(1)} %get-tuple-element.7), channel_id=1, source_target_pairs={{0,2},{1,3},{2,0},{3,1},{4,6},{5,7},{6,4},{7,5},{8,10},{9,11},{10,... | collective-permute-start | bytes 589832 | tf_op jit(solution)/shard_map/ppermute | solution.py:109
  84.6 10.5 %collective-permute-start.4 = (bf16[4,4,3,16,128]{4,3,2,1,0:T(8,128)(2,1)S(1)}, bf16[4,4,3,16,128]{4,3,2,1,0:T(8,128)(2,1)S(1)}, u32[]{:S(2)}, u32[]{:S(2)}) collective-permute-start(bf16[4,4,3,16,128]{4,3,2,1,0:T(8,128)(2,1)S(1)} %get-tuple-element.6), channel_id=1, source_target_pairs={{0,3},{1,2},{2,1},{3,0},{4,7},{5,6},{6,5},{7,4},{8,11},{9,10},{10,... | collective-permute-start | bytes 589832 | tf_op jit(solution)/shard_map/ppermute | solution.py:109
  95.1 0.9 copy-start.1
Sparse Core Ops, SparseCore 0:
  31.6 33.9 all-reduce.3
